TPU v7x, 32 devices: a whole 2x2x4 slice. The times are simulated.
32 devices in a mesh: sector: 16 (over z, y, x), block: 2 (over core).
Axes of the slice: x: 2, y: 2, z: 4, core: 2. Of those that a mesh axis runs over, the one named last changes fastest.
Arguments:
- adjoint_prev: float32 [5, 16, 128, 128], P(None, 'block', 'sector'), may hold values from -6 to 6
- adjoint_source: float32 [5, 16, 128, 128], P(None, 'block', 'sector'), may hold values from -6 to 6
- face_matrices: bfloat16 [3, 5, 5, 16, 128, 128], P(None, None, None, 'block', 'sector'), may hold values from -2.5 to 2.5
- inverse_blocks: bfloat16 [5, 5, 16, 128, 128], P(None, None, 'block', 'sector')
- sector_offset: int32 [1], replicated, may hold values from 1 to 15
- donor_cells: int32 [128], P('sector'), may hold values from 0 to 7
- donor_weights: float32 [128], P('sector'), may hold values from 0.1 to 0.9
Outputs:
- adjoint: float32 [5, 16, 128, 128], P(None, 'block', 'sector')
- last_update: float32 [5, 16, 128, 128], P(None, 'block', 'sector')
All inputs are finite; a program needn't handle non-finite values.
Results may differ from a plain program's by a relative error of at most 0.0003.
Values sent between devices are 32-bit elements; how exact they have to be, the bound alone decides.
A program may use at most 64 MiB of HBM per device.

v0:
```python
import jax
import jax.numpy as jnp
from jax import lax
from jax.sharding import PartitionSpec as P

ITERS = 4


def passed_along(value, axis, steps):
    count = lax.axis_size(axis)
    pairs = [(source, (source + steps) % count) for source in range(count)]
    return lax.ppermute(value, axis, pairs)


def padded(cells, sides, width, closed):
    for axis, dim in sides:
        count = lax.axis_size(axis)
        ends = count if closed else count - 1
        head = lax.slice_in_dim(cells, 0, width, axis=dim)
        tail = lax.slice_in_dim(cells, cells.shape[dim] - width, cells.shape[dim], axis=dim)
        cells = jnp.concatenate(
            [
                lax.ppermute(tail, axis, [(i, (i + 1) % count) for i in range(ends)]),
                cells,
                lax.ppermute(head, axis, [((i + 1) % count, i) for i in range(ends)]),
            ],
            axis=dim,
        )
    return cells


def shards(
    adjoint_prev,
    adjoint_source,
    face_matrices,
    inverse_blocks,
    sector_offset,
    donor_cells,
    donor_weights,
):
    sectors = lax.axis_size("sector")
    blocks = lax.axis_size("block")
    block_index = lax.axis_index("block")
    cells_around = adjoint_prev.shape[2]
    offset_value = sector_offset[0]
    columns = jnp.arange(cells_around + 1, dtype=jnp.int32)
    first_hit = (columns[None, :] == donor_cells[:, None]).astype(jnp.float32)
    second_hit = (columns[None, :] == donor_cells[:, None] + 1).astype(jnp.float32)
    blend_table = donor_weights[:, None] * first_hit + (1.0 - donor_weights[:, None]) * second_hit
    adjoint = adjoint_prev
    last_update = jnp.zeros_like(adjoint_prev)
    for sweep_number in range(ITERS):
        beside_all = padded(adjoint, (("sector", 2),), 1, True)
        along = padded(adjoint, (("block", 1),), 1, False)
        sweep_lower_rim = along[:, 0]
        upper_rim = along[:, -1]
        around_minus = beside_all[:, :, :-2]
        around_plus = beside_all[:, :, 2:]
        following = passed_along(sweep_lower_rim[:, :1], "sector", -1)
        extended = jnp.concatenate([sweep_lower_rim, following], axis=1)
        moved_rows = extended
        for bit_number in range((sectors - 1).bit_length()):
            hopped = passed_along(moved_rows, "sector", 1 << bit_number)
            moved_rows = jnp.where(offset_value >> bit_number & 1 == 1, hopped, moved_rows)
        facing = jnp.einsum("jk,nkr->njr", blend_table, moved_rows, precision=lax.Precision.HIGHEST)
        sweep_lower_rim = jnp.where(block_index == blocks // 2, facing, sweep_lower_rim)
        axial_minus = jnp.concatenate([sweep_lower_rim[:, None], adjoint[:, :-1]], axis=1)
        axial_plus = jnp.concatenate([adjoint[:, 1:], upper_rim[:, None]], axis=1)
        radial_pad = jnp.pad(adjoint, ((0, 0), (0, 0), (0, 0), (1, 1)))
        mixed = (
            0.6 * axial_minus + 0.4 * axial_plus,
            0.6 * around_minus + 0.4 * around_plus,
            0.6 * radial_pad[:, :, :, :-2] + 0.4 * radial_pad[:, :, :, 2:],
        )
        coupled = jnp.zeros_like(adjoint)
        for direction in range(3):
            for comp in range(5):
                coupled = (
                    coupled
                    + face_matrices[direction, comp].astype(jnp.float32)
                    * mixed[direction][comp][None]
                )
        total = adjoint_source + coupled
        result = jnp.zeros_like(adjoint)
        for comp in range(5):
            result = result + inverse_blocks[:, comp].astype(jnp.float32) * total[comp][None]
        last_update = result - adjoint
        adjoint = result
    return (adjoint, last_update)


def solution(mesh):
    return jax.shard_map(
        shards,
        mesh=mesh,
        in_specs=(
            P(None, "block", "sector", None),
            P(None, "block", "sector", None),
            P(None, None, None, "block", "sector", None),
            P(None, None, "block", "sector", None),
            P(),
            P("sector"),
            P("sector"),
        ),
        out_specs=(P(None, "block", "sector", None), P(None, "block", "sector", None)),
        check_vma=False,
    )
```

profile of v0, /device:TPU:0, one launch (start us, length us, event | category | flops | bytes accessed | tf_op | source)
XLA Modules:
  0.0 140.0 jit_solution(11164335714284014732)
XLA Ops:
  1.4 2.4 %collective-permute-start = (f32[5,1,8,128]{3,2,0,1:T(8,128)S(1)}, f32[5,1,8,128]{3,2,0,1:T(8,128)S(1)}, u32[]{:S(2)}, u32[]{:S(2)}) collective-permute-start(f32[5,1,8,128]{3,2,0,1:T(8,128)S(1)} %get-tuple-element.108), channel_id=1, source_target_pairs={{0,1},{2,3},{4,5},{6,7},{8,9},{10,11},{12,13},{14,15},{16,17},{18,... | collective-permute-start | bytes 61448 | tf_op jit(solution)/shard_map/ppermute | solution.py:23
  3.8 1.3 collective-permute-start.6
  6.2 2.4 %collective-permute-start.7 = (f32[5,8,1,128]{3,2,0,1:T(1,128)S(1)}, f32[5,8,1,128]{3,2,0,1:T(1,128)S(1)}, u32[]{:S(2)}, u32[]{:S(2)}) collective-permute-start(f32[5,8,1,128]{3,2,0,1:T(1,128)S(1)} %get-tuple-element.116), channel_id=1, source_target_pairs={{0,2},{2,4},{4,6},{6,8},{8,10},{10,12},{12,14},{14,16},{16,18},{18... | collective-permute-start | bytes 61448 | tf_op jit(solution)/shard_map/ppermute | solution.py:23
  8.5 4.1 %collective-permute-start.8 = (f32[5,8,1,128]{3,2,0,1:T(1,128)S(1)}, f32[5,8,1,128]{3,2,0,1:T(1,128)S(1)}, u32[]{:S(2)}, u32[]{:S(2)}) collective-permute-start(f32[5,8,1,128]{3,2,0,1:T(1,128)S(1)} %get-tuple-element.117), channel_id=1, source_target_pairs={{2,0},{4,2},{6,4},{8,6},{10,8},{12,10},{14,12},{16,14},{18,16},{20... | collective-permute-start | bytes 61448 | tf_op jit(solution)/shard_map/ppermute | solution.py:25
  13.6 2.0 %collective-permute-start.1 = (f32[5,1,128]{2,1,0:T(1,128)S(1)}, f32[5,1,128]{2,1,0:T(1,128)S(1)}, u32[]{:S(2)}, u32[]{:S(2)}) collective-permute-start(f32[5,1,128]{2,1,0:T(1,128)S(1)} %slice.645), channel_id=1, source_target_pairs={{0,30},{2,0},{4,2},{6,4},{8,6},{10,8},{12,10},{14,12},{16,14},{18,... | collective-permute-start | bytes 7688 | tf_op jit(solution)/shard_map/ppermute | solution.py:12
  17.9 6.9 %collective-permute-done.2 = f32[5,9,128]{2,1,0:T(8,128)S(1)} collective-permute-done((f32[5,9,128]{2,1,0:T(8,128)S(1)}, f32[5,9,128]{2,1,0:T(8,128)S(1)}, u32[]{:S(2)}, u32[]{:S(2)}) %collective-permute-start.2) | collective-permute-done | bytes 23072 | tf_op jit(solution)/shard_map/ppermute | solution.py:12
  25.0 6.7 %collective-permute-done.3 = f32[5,9,128]{2,1,0:T(8,128)S(1)} collective-permute-done((f32[5,9,128]{2,1,0:T(8,128)S(1)}, f32[5,9,128]{2,1,0:T(8,128)S(1)}, u32[]{:S(2)}, u32[]{:S(2)}) %collective-permute-start.3) | collective-permute-done | bytes 23072 | tf_op jit(solution)/shard_map/ppermute | solution.py:12
  31.9 5.6 %collective-permute-done.4 = f32[5,9,128]{2,1,0:T(8,128)S(1)} collective-permute-done((f32[5,9,128]{2,1,0:T(8,128)S(1)}, f32[5,9,128]{2,1,0:T(8,128)S(1)}, u32[]{:S(2)}, u32[]{:S(2)}) %collective-permute-start.4) | collective-permute-done | bytes 23072 | tf_op jit(solution)/shard_map/ppermute | solution.py:12
  37.6 4.9 %collective-permute-done.5 = f32[5,9,128]{2,1,0:T(8,128)S(1)} collective-permute-done((f32[5,9,128]{2,1,0:T(8,128)S(1)}, f32[5,9,128]{2,1,0:T(8,128)S(1)}, u32[]{:S(2)}, u32[]{:S(2)}) %collective-permute-start.5) | collective-permute-done | bytes 23072 | tf_op jit(solution)/shard_map/ppermute | solution.py:12
  45.3 3.6 %collective-permute-done.10 = f32[5,1,128]{2,1,0:T(1,128)S(1)} collective-permute-done((f32[5,1,128]{2,1,0:T(1,128)S(1)}, f32[5,1,128]{2,1,0:T(1,128)S(1)}, u32[]{:S(2)}, u32[]{:S(2)}) %collective-permute-start.10) | collective-permute-done | bytes 2592 | tf_op jit(solution)/shard_map/ppermute | solution.py:12
  50.3 5.7 %collective-permute-start.17 = (f32[5,8,1,128]{3,2,0,1:T(1,128)S(1)}, f32[5,8,1,128]{3,2,0,1:T(1,128)S(1)}, u32[]{:S(2)}, u32[]{:S(2)}) collective-permute-start(f32[5,8,1,128]{3,2,0,1:T(1,128)S(1)} %get-tuple-element.89), channel_id=1, source_target_pairs={{2,0},{4,2},{6,4},{8,6},{10,8},{12,10},{14,12},{16,14},{18,16},{20... | collective-permute-start | bytes 61448 | tf_op jit(solution)/shard_map/ppermute | solution.py:25
  57.8 5.4 %collective-permute-done.12 = f32[5,9,128]{2,1,0:T(8,128)S(1)} collective-permute-done((f32[5,9,128]{2,1,0:T(8,128)S(1)}, f32[5,9,128]{2,1,0:T(8,128)S(1)}, u32[]{:S(2)}, u32[]{:S(2)}) %collective-permute-start.12) | collective-permute-done | bytes 23072 | tf_op jit(solution)/shard_map/ppermute | solution.py:12
  63.3 6.1 %collective-permute-done.13 = f32[5,9,128]{2,1,0:T(8,128)S(1)} collective-permute-done((f32[5,9,128]{2,1,0:T(8,128)S(1)}, f32[5,9,128]{2,1,0:T(8,128)S(1)}, u32[]{:S(2)}, u32[]{:S(2)}) %collective-permute-start.13) | collective-permute-done | bytes 23072 | tf_op jit(solution)/shard_map/ppermute | solution.py:12
  69.4 4.9 %collective-permute-done.14 = f32[5,9,128]{2,1,0:T(8,128)S(1)} collective-permute-done((f32[5,9,128]{2,1,0:T(8,128)S(1)}, f32[5,9,128]{2,1,0:T(8,128)S(1)}, u32[]{:S(2)}, u32[]{:S(2)}) %collective-permute-start.14) | collective-permute-done | bytes 23072 | tf_op jit(solution)/shard_map/ppermute | solution.py:12
  77.1 3.6 %collective-permute-done.19 = f32[5,1,128]{2,1,0:T(1,128)S(1)} collective-permute-done((f32[5,1,128]{2,1,0:T(1,128)S(1)}, f32[5,1,128]{2,1,0:T(1,128)S(1)}, u32[]{:S(2)}, u32[]{:S(2)}) %collective-permute-start.19) | collective-permute-done | bytes 2592 | tf_op jit(solution)/shard_map/ppermute | solution.py:12
  82.1 5.7 %collective-permute-start.26 = (f32[5,8,1,128]{3,2,0,1:T(1,128)S(1)}, f32[5,8,1,128]{3,2,0,1:T(1,128)S(1)}, u32[]{:S(2)}, u32[]{:S(2)}) collective-permute-start(f32[5,8,1,128]{3,2,0,1:T(1,128)S(1)} %get-tuple-element.61), channel_id=1, source_target_pairs={{2,0},{4,2},{6,4},{8,6},{10,8},{12,10},{14,12},{16,14},{18,16},{20... | collective-permute-start | bytes 61448 | tf_op jit(solution)/shard_map/ppermute | solution.py:25
  89.7 5.4 %collective-permute-done.21 = f32[5,9,128]{2,1,0:T(8,128)S(1)} collective-permute-done((f32[5,9,128]{2,1,0:T(8,128)S(1)}, f32[5,9,128]{2,1,0:T(8,128)S(1)}, u32[]{:S(2)}, u32[]{:S(2)}) %collective-permute-start.21) | collective-permute-done | bytes 23072 | tf_op jit(solution)/shard_map/ppermute | solution.py:12
  95.1 6.1 %collective-permute-done.22 = f32[5,9,128]{2,1,0:T(8,128)S(1)} collective-permute-done((f32[5,9,128]{2,1,0:T(8,128)S(1)}, f32[5,9,128]{2,1,0:T(8,128)S(1)}, u32[]{:S(2)}, u32[]{:S(2)}) %collective-permute-start.22) | collective-permute-done | bytes 23072 | tf_op jit(solution)/shard_map/ppermute | solution.py:12
  101.2 4.9 %collective-permute-done.23 = f32[5,9,128]{2,1,0:T(8,128)S(1)} collective-permute-done((f32[5,9,128]{2,1,0:T(8,128)S(1)}, f32[5,9,128]{2,1,0:T(8,128)S(1)}, u32[]{:S(2)}, u32[]{:S(2)}) %collective-permute-start.23) | collective-permute-done | bytes 23072 | tf_op jit(solution)/shard_map/ppermute | solution.py:12
  109.0 3.6 %collective-permute-done.28 = f32[5,1,128]{2,1,0:T(1,128)S(1)} collective-permute-done((f32[5,1,128]{2,1,0:T(1,128)S(1)}, f32[5,1,128]{2,1,0:T(1,128)S(1)}, u32[]{:S(2)}, u32[]{:S(2)}) %collective-permute-start.28) | collective-permute-done | bytes 2592 | tf_op jit(solution)/shard_map/ppermute | solution.py:12
  114.0 5.7 %collective-permute-start.35 = (f32[5,8,1,128]{3,2,0,1:T(1,128)S(1)}, f32[5,8,1,128]{3,2,0,1:T(1,128)S(1)}, u32[]{:S(2)}, u32[]{:S(2)}) collective-permute-start(f32[5,8,1,128]{3,2,0,1:T(1,128)S(1)} %get-tuple-element.33), channel_id=1, source_target_pairs={{2,0},{4,2},{6,4},{8,6},{10,8},{12,10},{14,12},{16,14},{18,16},{20... | collective-permute-start | bytes 61448 | tf_op jit(solution)/shard_map/ppermute | solution.py:25
  121.5 5.4 %collective-permute-done.30 = f32[5,9,128]{2,1,0:T(8,128)S(1)} collective-permute-done((f32[5,9,128]{2,1,0:T(8,128)S(1)}, f32[5,9,128]{2,1,0:T(8,128)S(1)}, u32[]{:S(2)}, u32[]{:S(2)}) %collective-permute-start.30) | collective-permute-done | bytes 23072 | tf_op jit(solution)/shard_map/ppermute | solution.py:12
  126.9 6.1 %collective-permute-done.31 = f32[5,9,128]{2,1,0:T(8,128)S(1)} collective-permute-done((f32[5,9,128]{2,1,0:T(8,128)S(1)}, f32[5,9,128]{2,1,0:T(8,128)S(1)}, u32[]{:S(2)}, u32[]{:S(2)}) %collective-permute-start.31) | collective-permute-done | bytes 23072 | tf_op jit(solution)/shard_map/ppermute | solution.py:12
  133.1 4.9 %collective-permute-done.32 = f32[5,9,128]{2,1,0:T(8,128)S(1)} collective-permute-done((f32[5,9,128]{2,1,0:T(8,128)S(1)}, f32[5,9,128]{2,1,0:T(8,128)S(1)}, u32[]{:S(2)}, u32[]{:S(2)}) %collective-permute-start.32) | collective-permute-done | bytes 23072 | tf_op jit(solution)/shard_map/ppermute | solution.py:12
  (130 shorter events, 25.1 us)
Async XLA Ops:
  1.4 12.2 %collective-permute-start = (f32[5,1,8,128]{3,2,0,1:T(8,128)S(1)}, f32[5,1,8,128]{3,2,0,1:T(8,128)S(1)}, u32[]{:S(2)}, u32[]{:S(2)}) collective-permute-start(f32[5,1,8,128]{3,2,0,1:T(8,128)S(1)} %get-tuple-element.108), channel_id=1, source_target_pairs={{0,1},{2,3},{4,5},{6,7},{8,9},{10,11},{12,13},{14,15},{16,17},{18,... | collective-permute-start | bytes 61448 | tf_op jit(solution)/shard_map/ppermute | solution.py:23
  3.8 38.8 %collective-permute-start.6 = (f32[5,1,8,128]{3,2,0,1:T(8,128)S(1)}, f32[5,1,8,128]{3,2,0,1:T(8,128)S(1)}, u32[]{:S(2)}, u32[]{:S(2)}) collective-permute-start(f32[5,1,8,128]{3,2,0,1:T(8,128)S(1)} %get-tuple-element.107), channel_id=1, source_target_pairs={{1,0},{3,2},{5,4},{7,6},{9,8},{11,10},{13,12},{15,14},{17,16},{19,... | collective-permute-start | bytes 61448 | tf_op jit(solution)/shard_map/ppermute | solution.py:25
  6.2 25.5 %collective-permute-start.7 = (f32[5,8,1,128]{3,2,0,1:T(1,128)S(1)}, f32[5,8,1,128]{3,2,0,1:T(1,128)S(1)}, u32[]{:S(2)}, u32[]{:S(2)}) collective-permute-start(f32[5,8,1,128]{3,2,0,1:T(1,128)S(1)} %get-tuple-element.116), channel_id=1, source_target_pairs={{0,2},{2,4},{4,6},{6,8},{8,10},{10,12},{12,14},{14,16},{16,18},{18... | collective-permute-start | bytes 61448 | tf_op jit(solution)/shard_map/ppermute | solution.py:23
  8.5 23.2 %collective-permute-start.8 = (f32[5,8,1,128]{3,2,0,1:T(1,128)S(1)}, f32[5,8,1,128]{3,2,0,1:T(1,128)S(1)}, u32[]{:S(2)}, u32[]{:S(2)}) collective-permute-start(f32[5,8,1,128]{3,2,0,1:T(1,128)S(1)} %get-tuple-element.117), channel_id=1, source_target_pairs={{2,0},{4,2},{6,4},{8,6},{10,8},{12,10},{14,12},{16,14},{18,16},{20... | collective-permute-start | bytes 61448 | tf_op jit(solution)/shard_map/ppermute | solution.py:25
  17.3 7.6 %collective-permute-start.2 = (f32[5,9,128]{2,1,0:T(8,128)S(1)}, f32[5,9,128]{2,1,0:T(8,128)S(1)}, u32[]{:S(2)}, u32[]{:S(2)}) collective-permute-start(f32[5,9,128]{2,1,0:T(8,128)S(1)} %pad_maximum_fusion.8), channel_id=1, source_target_pairs={{0,2},{2,4},{4,6},{6,8},{8,10},{10,12},{12,14},{14,16},{16,18},{18... | collective-permute-start | bytes 69128 | tf_op jit(solution)/shard_map/ppermute | solution.py:12
  24.9 6.7 %collective-permute-start.3 = (f32[5,9,128]{2,1,0:T(8,128)S(1)}, f32[5,9,128]{2,1,0:T(8,128)S(1)}, u32[]{:S(2)}, u32[]{:S(2)}) collective-permute-start(f32[5,9,128]{2,1,0:T(8,128)S(1)} %broadcast_select_fusion.3), channel_id=1, source_target_pairs={{0,4},{2,6},{4,8},{6,10},{8,12},{10,14},{12,16},{14,18},{16,20},{1... | collective-permute-start | bytes 69128 | tf_op jit(solution)/shard_map/ppermute | solution.py:12
  48.9 7.6 %collective-permute-start.11 = (f32[5,9,128]{2,1,0:T(8,128)S(1)}, f32[5,9,128]{2,1,0:T(8,128)S(1)}, u32[]{:S(2)}, u32[]{:S(2)}) collective-permute-start(f32[5,9,128]{2,1,0:T(8,128)S(1)} %pad_maximum_fusion.9), channel_id=1, source_target_pairs={{0,2},{2,4},{4,6},{6,8},{8,10},{10,12},{12,14},{14,16},{16,18},{18... | collective-permute-start | bytes 69128 | tf_op jit(solution)/shard_map/ppermute | solution.py:12
  48.9 25.6 %collective-permute-start.15 = (f32[5,1,8,128]{3,2,0,1:T(8,128)S(1)}, f32[5,1,8,128]{3,2,0,1:T(8,128)S(1)}, u32[]{:S(2)}, u32[]{:S(2)}) collective-permute-start(f32[5,1,8,128]{3,2,0,1:T(8,128)S(1)} %get-tuple-element.79), channel_id=1, source_target_pairs={{1,0},{3,2},{5,4},{7,6},{9,8},{11,10},{13,12},{15,14},{17,16},{19,... | collective-permute-start | bytes 61448 | tf_op jit(solution)/shard_map/ppermute | solution.py:25
  50.2 7.4 %collective-permute-start.16 = (f32[5,8,1,128]{3,2,0,1:T(1,128)S(1)}, f32[5,8,1,128]{3,2,0,1:T(1,128)S(1)}, u32[]{:S(2)}, u32[]{:S(2)}) collective-permute-start(f32[5,8,1,128]{3,2,0,1:T(1,128)S(1)} %get-tuple-element.88), channel_id=1, source_target_pairs={{0,2},{2,4},{4,6},{6,8},{8,10},{10,12},{12,14},{14,16},{16,18},{18... | collective-permute-start | bytes 61448 | tf_op jit(solution)/shard_map/ppermute | solution.py:23
  50.3 7.4 %collective-permute-start.17 = (f32[5,8,1,128]{3,2,0,1:T(1,128)S(1)}, f32[5,8,1,128]{3,2,0,1:T(1,128)S(1)}, u32[]{:S(2)}, u32[]{:S(2)}) collective-permute-start(f32[5,8,1,128]{3,2,0,1:T(1,128)S(1)} %get-tuple-element.89), channel_id=1, source_target_pairs={{2,0},{4,2},{6,4},{8,6},{10,8},{12,10},{14,12},{16,14},{18,16},{20... | collective-permute-start | bytes 61448 | tf_op jit(solution)/shard_map/ppermute | solution.py:25
  56.5 6.7 %collective-permute-start.12 = (f32[5,9,128]{2,1,0:T(8,128)S(1)}, f32[5,9,128]{2,1,0:T(8,128)S(1)}, u32[]{:S(2)}, u32[]{:S(2)}) collective-permute-start(f32[5,9,128]{2,1,0:T(8,128)S(1)} %broadcast_select_fusion.2), channel_id=1, source_target_pairs={{0,4},{2,6},{4,8},{6,10},{8,12},{10,14},{12,16},{14,18},{16,20},{1... | collective-permute-start | bytes 69128 | tf_op jit(solution)/shard_map/ppermute | solution.py:12
  63.2 6.1 %collective-permute-start.13 = (f32[5,9,128]{2,1,0:T(8,128)S(1)}, f32[5,9,128]{2,1,0:T(8,128)S(1)}, u32[]{:S(2)}, u32[]{:S(2)}) collective-permute-start(f32[5,9,128]{2,1,0:T(8,128)S(1)} %broadcast_select_fusion.6), channel_id=1, source_target_pairs={{0,8},{2,10},{4,12},{6,14},{8,16},{10,18},{12,20},{14,22},{16,24},... | collective-permute-start | bytes 69128 | tf_op jit(solution)/shard_map/ppermute | solution.py:12
  80.7 7.6 %collective-permute-start.20 = (f32[5,9,128]{2,1,0:T(8,128)S(1)}, f32[5,9,128]{2,1,0:T(8,128)S(1)}, u32[]{:S(2)}, u32[]{:S(2)}) collective-permute-start(f32[5,9,128]{2,1,0:T(8,128)S(1)} %pad_maximum_fusion.10), channel_id=1, source_target_pairs={{0,2},{2,4},{4,6},{6,8},{8,10},{10,12},{12,14},{14,16},{16,18},{18... | collective-permute-start | bytes 69128 | tf_op jit(solution)/shard_map/ppermute | solution.py:12
  80.8 25.6 %collective-permute-start.24 = (f32[5,1,8,128]{3,2,0,1:T(8,128)S(1)}, f32[5,1,8,128]{3,2,0,1:T(8,128)S(1)}, u32[]{:S(2)}, u32[]{:S(2)}) collective-permute-start(f32[5,1,8,128]{3,2,0,1:T(8,128)S(1)} %get-tuple-element.51), channel_id=1, source_target_pairs={{1,0},{3,2},{5,4},{7,6},{9,8},{11,10},{13,12},{15,14},{17,16},{19,... | collective-permute-start | bytes 61448 | tf_op jit(solution)/shard_map/ppermute | solution.py:25
  82.1 7.4 %collective-permute-start.25 = (f32[5,8,1,128]{3,2,0,1:T(1,128)S(1)}, f32[5,8,1,128]{3,2,0,1:T(1,128)S(1)}, u32[]{:S(2)}, u32[]{:S(2)}) collective-permute-start(f32[5,8,1,128]{3,2,0,1:T(1,128)S(1)} %get-tuple-element.60), channel_id=1, source_target_pairs={{0,2},{2,4},{4,6},{6,8},{8,10},{10,12},{12,14},{14,16},{16,18},{18... | collective-permute-start | bytes 61448 | tf_op jit(solution)/shard_map/ppermute | solution.py:23
  82.1 7.4 %collective-permute-start.26 = (f32[5,8,1,128]{3,2,0,1:T(1,128)S(1)}, f32[5,8,1,128]{3,2,0,1:T(1,128)S(1)}, u32[]{:S(2)}, u32[]{:S(2)}) collective-permute-start(f32[5,8,1,128]{3,2,0,1:T(1,128)S(1)} %get-tuple-element.61), channel_id=1, source_target_pairs={{2,0},{4,2},{6,4},{8,6},{10,8},{12,10},{14,12},{16,14},{18,16},{20... | collective-permute-start | bytes 61448 | tf_op jit(solution)/shard_map/ppermute | solution.py:25
  88.3 6.7 %collective-permute-start.21 = (f32[5,9,128]{2,1,0:T(8,128)S(1)}, f32[5,9,128]{2,1,0:T(8,128)S(1)}, u32[]{:S(2)}, u32[]{:S(2)}) collective-permute-start(f32[5,9,128]{2,1,0:T(8,128)S(1)} %broadcast_select_fusion.1), channel_id=1, source_target_pairs={{0,4},{2,6},{4,8},{6,10},{8,12},{10,14},{12,16},{14,18},{16,20},{1... | collective-permute-start | bytes 69128 | tf_op jit(solution)/shard_map/ppermute | solution.py:12
  95.1 6.1 %collective-permute-start.22 = (f32[5,9,128]{2,1,0:T(8,128)S(1)}, f32[5,9,128]{2,1,0:T(8,128)S(1)}, u32[]{:S(2)}, u32[]{:S(2)}) collective-permute-start(f32[5,9,128]{2,1,0:T(8,128)S(1)} %broadcast_select_fusion.5), channel_id=1, source_target_pairs={{0,8},{2,10},{4,12},{6,14},{8,16},{10,18},{12,20},{14,22},{16,24},... | collective-permute-start | bytes 69128 | tf_op jit(solution)/shard_map/ppermute | solution.py:12
  112.5 7.6 %collective-permute-start.29 = (f32[5,9,128]{2,1,0:T(8,128)S(1)}, f32[5,9,128]{2,1,0:T(8,128)S(1)}, u32[]{:S(2)}, u32[]{:S(2)}) collective-permute-start(f32[5,9,128]{2,1,0:T(8,128)S(1)} %pad_maximum_fusion.11), channel_id=1, source_target_pairs={{0,2},{2,4},{4,6},{6,8},{8,10},{10,12},{12,14},{14,16},{16,18},{18... | collective-permute-start | bytes 69128 | tf_op jit(solution)/shard_map/ppermute | solution.py:12
  112.6 25.6 %collective-permute-start.33 = (f32[5,1,8,128]{3,2,0,1:T(8,128)S(1)}, f32[5,1,8,128]{3,2,0,1:T(8,128)S(1)}, u32[]{:S(2)}, u32[]{:S(2)}) collective-permute-start(f32[5,1,8,128]{3,2,0,1:T(8,128)S(1)} %get-tuple-element.23), channel_id=1, source_target_pairs={{1,0},{3,2},{5,4},{7,6},{9,8},{11,10},{13,12},{15,14},{17,16},{19,... | collective-permute-start | bytes 61448 | tf_op jit(solution)/shard_map/ppermute | solution.py:25
  113.9 7.4 %collective-permute-start.34 = (f32[5,8,1,128]{3,2,0,1:T(1,128)S(1)}, f32[5,8,1,128]{3,2,0,1:T(1,128)S(1)}, u32[]{:S(2)}, u32[]{:S(2)}) collective-permute-start(f32[5,8,1,128]{3,2,0,1:T(1,128)S(1)} %get-tuple-element.32), channel_id=1, source_target_pairs={{0,2},{2,4},{4,6},{6,8},{8,10},{10,12},{12,14},{14,16},{16,18},{18... | collective-permute-start | bytes 61448 | tf_op jit(solution)/shard_map/ppermute | solution.py:23
  114.0 7.4 %collective-permute-start.35 = (f32[5,8,1,128]{3,2,0,1:T(1,128)S(1)}, f32[5,8,1,128]{3,2,0,1:T(1,128)S(1)}, u32[]{:S(2)}, u32[]{:S(2)}) collective-permute-start(f32[5,8,1,128]{3,2,0,1:T(1,128)S(1)} %get-tuple-element.33), channel_id=1, source_target_pairs={{2,0},{4,2},{6,4},{8,6},{10,8},{12,10},{14,12},{16,14},{18,16},{20... | collective-permute-start | bytes 61448 | tf_op jit(solution)/shard_map/ppermute | solution.py:25
  120.2 6.7 %collective-permute-start.30 = (f32[5,9,128]{2,1,0:T(8,128)S(1)}, f32[5,9,128]{2,1,0:T(8,128)S(1)}, u32[]{:S(2)}, u32[]{:S(2)}) collective-permute-start(f32[5,9,128]{2,1,0:T(8,128)S(1)} %broadcast_select_fusion), channel_id=1, source_target_pairs={{0,4},{2,6},{4,8},{6,10},{8,12},{10,14},{12,16},{14,18},{16,20},{1... | collective-permute-start | bytes 69128 | tf_op jit(solution)/shard_map/ppermute | solution.py:12
  126.9 6.1 %collective-permute-start.31 = (f32[5,9,128]{2,1,0:T(8,128)S(1)}, f32[5,9,128]{2,1,0:T(8,128)S(1)}, u32[]{:S(2)}, u32[]{:S(2)}) collective-permute-start(f32[5,9,128]{2,1,0:T(8,128)S(1)} %broadcast_select_fusion.4), channel_id=1, source_target_pairs={{0,8},{2,10},{4,12},{6,14},{8,16},{10,18},{12,20},{14,22},{16,24},... | collective-permute-start | bytes 69128 | tf_op jit(solution)/shard_map/ppermute | solution.py:12
  (17 other events, 140.5 us)
where the time goes:
time: 140 us
  waiting for transfers between devices  91.8 us (66%)
  starting transfers between devices  37.3 us (27%)
  local copies, waits for them, and re-layouts  5.66 us (4%)
  other arithmetic  2.37 us (2%)
  between operations  1.96 us (1%)
    ppermute x20, waiting for transfers between devices, passed_along(): return lax.ppermute(value, axis, pairs)  86 us
    ppermute x8, starting transfers between devices, padded(): lax.ppermute(head, axis, [((i + 1) % count, i) for i in range(ends)])  26.2 us
    ppermute x8, starting transfers between devices, padded(): lax.ppermute(tail, axis, [(i, (i + 1) % count) for i in range(ends)])  8.8 us
    ppermute x8, waiting for transfers between devices, padded(): lax.ppermute(tail, axis, [(i, (i + 1) % count) for i in range(ends)])  5.8 us
  transfers between devices with their start and end apart: 36, of which 26 were waited for; matrix products, arithmetic and copies ran while one was open for 4% of the time, Pallas kernels for 0%

commit v1 on v0

v1 whole, which is shorter than its diff:
```python
import functools

import jax
import jax.numpy as jnp
from jax import lax
from jax.experimental import pallas as pl
from jax.experimental.pallas import tpu as pltpu
from jax.sharding import PartitionSpec as P

ITERS = 4
MESH = pl.DeviceIdType.MESH


def low_part(sectors):
    return max(d for d in range(1, sectors + 1) if sectors % d == 0 and d * d <= sectors)


def kernel(
    sectors,
    blocks,
    prev_ref,
    source_ref,
    face_ref,
    inverse_ref,
    offset_ref,
    cells_ref,
    weights_ref,
    adjoint_ref,
    update_ref,
    field,
    source,
    face16,
    inverse16,
    face,
    inverse,
    partial,
    edge,
    halo,
    rows,
    forward,
    picked,
    blend,
    local_sem,
    edge_send,
    edge_recv,
    rim_send,
    rim_recv,
    row_send,
    row_recv,
    forward_send,
    forward_recv,
):
    comps, layers, around, lanes = prev_ref.shape
    sector = lax.axis_index("sector")
    block = lax.axis_index("block")
    first = blocks // 2
    lows = low_part(sectors)
    highs = sectors // lows
    high, low = sector // lows, sector % lows
    after, before = (sector + 1) % sectors, (sector + sectors - 1) % sectors
    is_stator_face = block == first
    is_rotor_face = block == first - 1

    barrier = pltpu.get_barrier_semaphore()

    def greet(to_sector, to_block):
        pl.semaphore_signal(barrier, inc=1, device_id=(to_sector, to_block), device_id_type=MESH)

    greet(after, block)
    greet(before, block)

    @pl.when(block > 0)
    def _():
        greet(sector, block - 1)

    @pl.when(block < blocks - 1)
    def _():
        greet(sector, block + 1)

    @pl.when(is_rotor_face)
    def _():
        for step in range(highs):
            greet(((high + step) % highs) * lows + low, first)

    @pl.when(is_stator_face)
    def _():
        for step in range(highs):
            greet(((high + step) % highs) * lows + low, first - 1)
        for step in range(1, lows):
            greet(high * lows + (low + step) % lows, first)

    into_field = pltpu.make_async_copy(prev_ref, field.at[0, :, pl.ds(1, layers)], local_sem.at[0])
    into_source = pltpu.make_async_copy(source_ref, source, local_sem.at[1])
    into_face = pltpu.make_async_copy(face_ref, face16, local_sem.at[2])
    into_inverse = pltpu.make_async_copy(inverse_ref, inverse16, local_sem.at[3])
    for copy in (into_field, into_source, into_face, into_inverse):
        copy.start()

    @pl.when(block == 0)
    def _():
        for k in range(ITERS):
            for n in range(comps):
                field[k, n, 0] = jnp.zeros((around, lanes), jnp.float32)

    @pl.when(block == blocks - 1)
    def _():
        for k in range(ITERS):
            for n in range(comps):
                field[k, n, layers + 1] = jnp.zeros((around, lanes), jnp.float32)

    column = lax.broadcasted_iota(jnp.int32, (around, lanes), 0)
    lane = lax.broadcasted_iota(jnp.int32, (around, lanes), 1)
    donor = jnp.zeros((around, lanes), jnp.int32)
    weight = jnp.zeros((around, lanes), jnp.float32)
    for j in range(around):
        donor = jnp.where(column == j, cells_ref[j], donor)
        weight = jnp.where(column == j, weights_ref[j], weight)
    for k in range(around + 1):
        blend[k] = jnp.where(donor == k, weight, 0.0) + jnp.where(donor + 1 == k, 1.0 - weight, 0.0)
    radial_lower = jnp.where(lane == 0, 0.0, 0.6).astype(jnp.float32)
    radial_upper = jnp.where(lane == lanes - 1, 0.0, 0.4).astype(jnp.float32)

    into_field.wait()
    for n in range(comps):
        edge[0, 0, n] = field[0, n, pl.ds(1, layers), around - 1, :]
        edge[0, 1, n] = field[0, n, pl.ds(1, layers), 0, :]

    def edge_copy(k, side):
        return pltpu.make_async_remote_copy(
            src_ref=edge.at[k, side],
            dst_ref=halo.at[k, side],
            send_sem=edge_send.at[k, side],
            recv_sem=edge_recv.at[k, side],
            device_id=(before if side else after, block),
            device_id_type=MESH,
        )

    def rim_copy(k, side):
        return pltpu.make_async_remote_copy(
            src_ref=field.at[k, :, 1 if side else layers],
            dst_ref=field.at[k, :, layers + 1 if side else 0],
            send_sem=rim_send.at[k, side],
            recv_sem=rim_recv.at[k, side],
            device_id=(sector, block - 1 if side else block + 1),
            device_id_type=MESH,
        )

    def row_copy(k, step):
        to = (high + step) % highs
        return pltpu.make_async_remote_copy(
            src_ref=field.at[k, :, layers],
            dst_ref=rows[k].at[high],
            send_sem=row_send.at[k, step],
            recv_sem=row_recv.at[k, step],
            device_id=(to * lows + low, first),
            device_id_type=MESH,
        )

    def row_arrival(k, step):
        origin = (high + highs - step) % highs
        return pltpu.make_async_remote_copy(
            src_ref=field.at[k, :, layers],
            dst_ref=rows[k].at[origin],
            send_sem=row_send.at[k, step],
            recv_sem=row_recv.at[k, step],
            device_id=(origin * lows + low, first),
            device_id_type=MESH,
        )

    def forward_copy(k, step):
        return pltpu.make_async_remote_copy(
            src_ref=forward.at[k],
            dst_ref=picked[k].at[low],
            send_sem=forward_send.at[k, step],
            recv_sem=forward_recv.at[k, step],
            device_id=(high * lows + (low + step) % lows, first),
            device_id_type=MESH,
        )

    def forward_arrival(k, step):
        origin = (low + lows - step) % lows
        return pltpu.make_async_remote_copy(
            src_ref=forward.at[k],
            dst_ref=picked[k].at[origin],
            send_sem=forward_send.at[k, step],
            recv_sem=forward_recv.at[k, step],
            device_id=(high * lows + origin, first),
            device_id_type=MESH,
        )

    def send_rows(k):
        @pl.when(is_rotor_face)
        def _():
            for step in reversed(range(highs)):
                row_copy(k, step).start()

    def send_rims(k):
        @pl.when(block > 0)
        def _():
            rim_copy(k, 1).start()

        @pl.when((block < blocks - 1) & (block != first - 1))
        def _():
            rim_copy(k, 0).start()

    greetings = 2 + (block > 0).astype(jnp.int32) + (block < blocks - 1).astype(jnp.int32)
    greetings += jnp.where(is_rotor_face, highs, 0) + jnp.where(is_stator_face, highs + lows - 1, 0)
    pl.semaphore_wait(barrier, greetings)

    edge_copy(0, 0).start()
    edge_copy(0, 1).start()
    send_rows(0)
    send_rims(0)

    into_face.wait()

    def widen(i, carry):
        for d in range(3):
            for m in range(comps):
                face[d, i, m] = face16[d, i, m].astype(jnp.float32)
        return carry

    lax.fori_loop(0, comps, widen, 0)
    into_inverse.wait()

    def widen_inverse(i, carry):
        for m in range(comps):
            inverse[i, m] = inverse16[i, m].astype(jnp.float32)
        return carry

    lax.fori_loop(0, comps, widen_inverse, 0)
    into_source.wait()

    def radial(k, a, acc):
        for n in range(comps):
            here = field[k, n, a + 1]
            mix = radial_lower * pltpu.roll(here, 1, 1) + radial_upper * pltpu.roll(here, lanes - 1, 1)
            acc = [acc[m] + face[2, n, m, a] * mix for m in range(comps)]
        return acc

    def axial(k, a, acc):
        for n in range(comps):
            mix = 0.6 * field[k, n, a] + 0.4 * field[k, n, a + 2]
            acc = [acc[m] + face[0, n, m, a] * mix for m in range(comps)]
        return acc

    def circumferential(k, a, acc):
        for n in range(comps):
            here = field[k, n, a + 1]
            minus = jnp.where(column == 0, halo[k, 0, n, pl.ds(a, 1), :], pltpu.roll(here, 1, 0))
            plus = jnp.where(column == around - 1, halo[k, 1, n, pl.ds(a, 1), :], pltpu.roll(here, around - 1, 0))
            mix = 0.6 * minus + 0.4 * plus
            acc = [acc[m] + face[1, n, m, a] * mix for m in range(comps)]
        return acc

    def early(k, a, rim):
        acc = radial(k, a, [source[m, a] for m in range(comps)])
        if not rim:
            acc = axial(k, a, acc)
        for m in range(comps):
            partial[m, a] = acc[m]

    def late(k, a, rim):
        acc = circumferential(k, a, [partial[m, a] for m in range(comps)])
        if rim:
            acc = axial(k, a, acc)
        for m in range(comps):
            fresh = inverse[m, 0, a] * acc[0]
            for n in range(1, comps):
                fresh = fresh + inverse[m, n, a] * acc[n]
            if k < ITERS - 1:
                field[k + 1, m, a + 1] = fresh
                edge[k + 1, 0, m, pl.ds(a, 1), :] = fresh[around - 1 :, :]
                edge[k + 1, 1, m, pl.ds(a, 1), :] = fresh[:1, :]
            else:
                adjoint_ref[m, a] = fresh
                update_ref[m, a] = fresh - field[k, m, a + 1]

    offset = offset_ref[0]
    offset_high, offset_low = offset // lows, offset % lows

    def face_the_rotor(k):
        for step in range(highs):
            row_arrival(k, step).wait_recv()
        whole_from = (high + 2 * highs - offset_high - (low + offset_low) // lows) % highs
        first_from = (high + 2 * highs + 1 - offset_high - (low + offset_low + lows - 1) // lows) % highs
        for n in range(comps):
            forward[k, n] = rows[k][whole_from, n]
            forward[k, comps, n : n + 1, :] = rows[k][first_from, n, 0:1, :]
        for step in range(1, lows):
            forward_copy(k, step).start()
        for n in range(comps + 1):
            picked[k][low, n] = forward[k, n]
        for step in range(1, lows):
            forward_arrival(k, step).wait_recv()
        row_of = (low + lows - offset_low) % lows
        next_of = (low + lows - offset_low + 1) % lows
        for n in range(comps):
            total = blend[around] * picked[k][next_of, comps, n : n + 1, :]
            for c in range(around):
                total = total + blend[c] * picked[k][row_of, n, c : c + 1, :]
            field[k, n, 0] = total

    def body_of(step, k, rim):
        def body(a, carry):
            step(k, a, rim)
            return carry

        return body

    for k in range(ITERS):
        lax.fori_loop(1, layers - 1, body_of(early, k, False), 0)
        early(k, 0, True)
        early(k, layers - 1, True)
        edge_copy(k, 0).wait_recv()
        edge_copy(k, 1).wait_recv()
        lax.fori_loop(1, layers - 1, body_of(late, k, False), 0)

        @pl.when(block < blocks - 1)
        def _():
            rim_copy(k, 1).wait_recv()

        @pl.when((block > 0) & (block != first))
        def _():
            rim_copy(k, 0).wait_recv()

        @pl.when(is_stator_face)
        def _():
            face_the_rotor(k)

        late(k, layers - 1, True)
        late(k, 0, True)
        if k < ITERS - 1:
            edge_copy(k + 1, 0).start()
            edge_copy(k + 1, 1).start()
            send_rows(k + 1)
            send_rims(k + 1)

    for k in range(ITERS):
        edge_copy(k, 0).wait_send()
        edge_copy(k, 1).wait_send()

        @pl.when(block > 0)
        def _():
            rim_copy(k, 1).wait_send()

        @pl.when((block < blocks - 1) & (block != first - 1))
        def _():
            rim_copy(k, 0).wait_send()

        @pl.when(is_rotor_face)
        def _():
            for step in range(highs):
                row_copy(k, step).wait_send()

        @pl.when(is_stator_face)
        def _():
            for step in range(1, lows):
                forward_copy(k, step).wait_send()


def solution(mesh):
    sectors, blocks = mesh.shape["sector"], mesh.shape["block"]
    lows = low_part(sectors)
    highs = sectors // lows

    def sweeps(prev, source, face, inverse, offset, cells, weights):
        comps, layers, around, lanes = prev.shape
        f32, dma = jnp.float32, pltpu.SemaphoreType.DMA
        plane = (around, lanes)
        hbm = pl.BlockSpec(memory_space=pl.ANY)
        smem = pl.BlockSpec(memory_space=pltpu.SMEM)
        vmem = pl.BlockSpec(memory_space=pltpu.VMEM)
        return pl.pallas_call(
            functools.partial(kernel, sectors, blocks),
            out_shape=(pltpu.VMEM(prev.shape, f32),) * 2,
            in_specs=[hbm] * 4 + [smem] * 3,
            out_specs=(vmem, vmem),
            scratch_shapes=[
                pltpu.VMEM((ITERS, comps, layers + 2) + plane, f32),
                pltpu.VMEM(prev.shape, f32),
                pltpu.VMEM(face.shape, face.dtype),
                pltpu.VMEM(inverse.shape, inverse.dtype),
                pltpu.VMEM(face.shape, f32),
                pltpu.VMEM(inverse.shape, f32),
                pltpu.VMEM(prev.shape, f32),
                pltpu.VMEM((ITERS, 2, comps, layers, lanes), f32),
                pltpu.VMEM((ITERS, 2, comps, layers, lanes), f32),
                [pltpu.VMEM((highs, comps) + plane, f32)] * ITERS,
                pltpu.VMEM((ITERS, comps + 1) + plane, f32),
                [pltpu.VMEM((lows, comps + 1) + plane, f32)] * ITERS,
                pltpu.VMEM((around + 1,) + plane, f32),
                dma((4,)),
                dma((ITERS, 2)),
                dma((ITERS, 2)),
                dma((ITERS, 2)),
                dma((ITERS, 2)),
                dma((ITERS, highs)),
                dma((ITERS, highs)),
                dma((ITERS, lows)),
                dma((ITERS, lows)),
            ],
            compiler_params=pltpu.CompilerParams(collective_id=0, has_side_effects=True),
        )(prev, source, face, inverse, offset, cells, weights)

    return jax.shard_map(
        sweeps,
        mesh=mesh,
        in_specs=(
            P(None, "block", "sector", None),
            P(None, "block", "sector", None),
            P(None, None, None, "block", "sector", None),
            P(None, None, "block", "sector", None),
            P(),
            P("sector"),
            P("sector"),
        ),
        out_specs=(P(None, "block", "sector", None), P(None, "block", "sector", None)),
        check_vma=False,
    )
```

time: 140 us -> 34.5 us (0.25)
  the two profiles are of different devices: /device:TPU:0 before, /device:TPU:1 now
where the time goes in v1:
time: 34.5 us; the launch traced here: 34.3 us
  Pallas kernels  31.7 us (92%)
  local copies, waits for them, and re-layouts  1.33 us (4%)
  between operations  1.29 us (4%)
    pallas_call x1, Pallas kernels, sweeps(): pl.pallas_call(functools.partial(kernel, sectors, blocks), out_shape=(plt...  31.7 us
    unnamed x2, local copies, waits for them, and re-layouts  1.33 us

profile of v1, /device:TPU:1, one launch (start us, length us, event | category | flops | bytes accessed | tf_op | source)
XLA Modules:
  0.0 34.3 jit_solution(13295100759435942550)
XLA Ops:
  1.3 31.7 %shard_map.86 = (f32[5,8,8,128]{3,2,1,0:T(8,128)S(1)}, f32[5,8,8,128]{3,2,1,0:T(8,128)S(1)}) custom-call(f32[5,8,8,128]{3,2,1,0:T(8,128)} %prev_ref.1, f32[5,8,8,128]{3,2,1,0:T(8,128)} %source_ref.1, bf16[3,5,5,8,8,128]{5,4,3,2,1,0:T(8,128)(2,1)} %face_ref.1, bf16[5,5,8,8,128]{4,3,2,1,0:T(8,128)(2,1)} %inverse_ref.1, s32[1]{0:T(128)S(6)} %copy.13.offset_ref, ...), custom_call_target="tpu_custom_call" | custom-call | tf_op jit(solution)/shard_map/pallas_call | solution.py:374
  32.9 0.7 %copy.11 = f32[5,8,8,128]{3,2,1,0:T(8,128)} copy(f32[5,8,8,128]{3,2,1,0:T(8,128)S(1)} %get-tuple-element.2) | data formatting | bytes 327680
  33.6 0.7 %copy.12 = f32[5,8,8,128]{3,2,1,0:T(8,128)} copy(f32[5,8,8,128]{3,2,1,0:T(8,128)S(1)} %get-tuple-element.3) | data formatting | bytes 327680

commit v2 on v1

--- a/solution.py
+++ b/solution.py
@@ -22,11 +22,14 @@
     source_ref,
     face_ref,
     inverse_ref,
+    offset_hbm,
+    cells_hbm,
+    weights_hbm,
+    adjoint_ref,
+    update_ref,
     offset_ref,
     cells_ref,
     weights_ref,
-    adjoint_ref,
-    update_ref,
     field,
     source,
     face16,
@@ -40,6 +43,10 @@
     forward,
     picked,
     blend,
+    face_edge,
+    inverse_edge,
+    source_edge,
+    partial_edge,
     local_sem,
     edge_send,
     edge_recv,
@@ -93,7 +100,11 @@
     into_source = pltpu.make_async_copy(source_ref, source, local_sem.at[1])
     into_face = pltpu.make_async_copy(face_ref, face16, local_sem.at[2])
     into_inverse = pltpu.make_async_copy(inverse_ref, inverse16, local_sem.at[3])
-    for copy in (into_field, into_source, into_face, into_inverse):
+    into_offset = pltpu.make_async_copy(offset_hbm, offset_ref, local_sem.at[4])
+    into_cells = pltpu.make_async_copy(cells_hbm, cells_ref, local_sem.at[5])
+    into_weights = pltpu.make_async_copy(weights_hbm, weights_ref, local_sem.at[6])
+    scalars = (into_offset, into_cells, into_weights)
+    for copy in (into_field,) + scalars + (into_face, into_inverse, into_source):
         copy.start()
 
     @pl.when(block == 0)
@@ -108,6 +119,8 @@
             for n in range(comps):
                 field[k, n, layers + 1] = jnp.zeros((around, lanes), jnp.float32)
 
+    for copy in scalars:
+        copy.wait()
     column = lax.broadcasted_iota(jnp.int32, (around, lanes), 0)
     lane = lax.broadcasted_iota(jnp.int32, (around, lanes), 1)
     donor = jnp.zeros((around, lanes), jnp.int32)
@@ -213,11 +226,14 @@
     send_rims(0)
 
     into_face.wait()
+    rims = (around - 1, 0)
 
     def widen(i, carry):
         for d in range(3):
             for m in range(comps):
                 face[d, i, m] = face16[d, i, m].astype(jnp.float32)
+                for side in range(2):
+                    face_edge[d, side, i, m] = face[d, i, m, :, rims[side], :]
         return carry
 
     lax.fori_loop(0, comps, widen, 0)
@@ -226,10 +242,47 @@
     def widen_inverse(i, carry):
         for m in range(comps):
             inverse[i, m] = inverse16[i, m].astype(jnp.float32)
+            for side in range(2):
+                inverse_edge[side, i, m] = inverse[i, m, :, rims[side], :]
         return carry
 
     lax.fori_loop(0, comps, widen_inverse, 0)
     into_source.wait()
+    for side in range(2):
+        for m in range(comps):
+            source_edge[side, m] = source[m, :, rims[side], :]
+
+    edge_lane = lax.broadcasted_iota(jnp.int32, (layers, lanes), 1)
+    edge_lower = jnp.where(edge_lane == 0, 0.0, 0.6).astype(jnp.float32)
+    edge_upper = jnp.where(edge_lane == lanes - 1, 0.0, 0.4).astype(jnp.float32)
+
+    def early_edge(k, side):
+        inner, share = (around - 2, 0.6) if side == 0 else (1, 0.4)
+        acc = [source_edge[side, m] for m in range(comps)]
+        for n in range(comps):
+            own = edge[k, side, n]
+            mix = edge_lower * pltpu.roll(own, 1, 1) + edge_upper * pltpu.roll(own, lanes - 1, 1)
+            beside = share * field[k, n, pl.ds(1, layers), inner, :]
+            for m in range(comps):
+                acc[m] = acc[m] + face_edge[2, side, n, m] * mix + face_edge[1, side, n, m] * beside
+        for m in range(comps):
+            partial_edge[side, m] = acc[m]
+
+    def late_edge(k, side):
+        share = 0.4 if side == 0 else 0.6
+        acc = [partial_edge[side, m] for m in range(comps)]
+        for n in range(comps):
+            lower = field[k, n, pl.ds(0, layers), rims[side], :]
+            upper = field[k, n, pl.ds(2, layers), rims[side], :]
+            mix = 0.6 * lower + 0.4 * upper
+            beside = share * halo[k, 1 - side, n]
+            for m in range(comps):
+                acc[m] = acc[m] + face_edge[0, side, n, m] * mix + face_edge[1, side, n, m] * beside
+        for m in range(comps):
+            fresh = inverse_edge[side, m, 0] * acc[0]
+            for n in range(1, comps):
+                fresh = fresh + inverse_edge[side, m, n] * acc[n]
+            edge[k + 1, side, m] = fresh
 
     def radial(k, a, acc):
         for n in range(comps):
@@ -260,18 +313,27 @@
         for m in range(comps):
             partial[m, a] = acc[m]
 
+    def middle(k, a):
+        acc = circumferential(k, a, [partial[m, a] for m in range(comps)])
+        for m in range(comps):
+            partial[m, a] = acc[m]
+
+    def finish(k, a):
+        store(k, a, axial(k, a, [partial[m, a] for m in range(comps)]))
+
     def late(k, a, rim):
         acc = circumferential(k, a, [partial[m, a] for m in range(comps)])
         if rim:
             acc = axial(k, a, acc)
+        store(k, a, acc)
+
+    def store(k, a, acc):
         for m in range(comps):
             fresh = inverse[m, 0, a] * acc[0]
             for n in range(1, comps):
                 fresh = fresh + inverse[m, n, a] * acc[n]
             if k < ITERS - 1:
                 field[k + 1, m, a + 1] = fresh
-                edge[k + 1, 0, m, pl.ds(a, 1), :] = fresh[around - 1 :, :]
-                edge[k + 1, 1, m, pl.ds(a, 1), :] = fresh[:1, :]
             else:
                 adjoint_ref[m, a] = fresh
                 update_ref[m, a] = fresh - field[k, m, a + 1]
@@ -279,7 +341,7 @@
     offset = offset_ref[0]
     offset_high, offset_low = offset // lows, offset % lows
 
-    def face_the_rotor(k):
+    def pass_rows_on(k):
         for step in range(highs):
             row_arrival(k, step).wait_recv()
         whole_from = (high + 2 * highs - offset_high - (low + offset_low) // lows) % highs
@@ -291,6 +353,8 @@
             forward_copy(k, step).start()
         for n in range(comps + 1):
             picked[k][low, n] = forward[k, n]
+
+    def face_the_rotor(k):
         for step in range(1, lows):
             forward_arrival(k, step).wait_recv()
         row_of = (low + lows - offset_low) % lows
@@ -309,32 +373,73 @@
         return body
 
     for k in range(ITERS):
+        last = k == ITERS - 1
         lax.fori_loop(1, layers - 1, body_of(early, k, False), 0)
         early(k, 0, True)
         early(k, layers - 1, True)
+        if not last:
+            early_edge(k, 0)
+            early_edge(k, 1)
+
+        @pl.when(is_stator_face)
+        def _():
+            pass_rows_on(k)
+
         edge_copy(k, 0).wait_recv()
         edge_copy(k, 1).wait_recv()
-        lax.fori_loop(1, layers - 1, body_of(late, k, False), 0)
+        if last:
+            lax.fori_loop(1, layers - 1, body_of(late, k, False), 0)
+            middle(k, 0)
 
         @pl.when(block < blocks - 1)
         def _():
             rim_copy(k, 1).wait_recv()
 
+        @pl.when(is_rotor_face)
+        def _():
+            late(k, layers - 1, True)
+
         @pl.when((block > 0) & (block != first))
         def _():
             rim_copy(k, 0).wait_recv()
 
+        if last:
+
+            @pl.when(block != first - 1)
+            def _():
+                late(k, layers - 1, True)
+
         @pl.when(is_stator_face)
         def _():
             face_the_rotor(k)
 
-        late(k, layers - 1, True)
-        late(k, 0, True)
-        if k < ITERS - 1:
-            edge_copy(k + 1, 0).start()
-            edge_copy(k + 1, 1).start()
-            send_rows(k + 1)
-            send_rims(k + 1)
+        if last:
+            finish(k, 0)
+        else:
+            for side in range(2):
+                late_edge(k, side)
+                edge_copy(k + 1, side).start()
+
+            @pl.when(is_rotor_face)
+            def _():
+                for step in reversed(range(highs)):
+                    row_copy(k + 1, step).start()
+
+            late(k, 0, True)
+
+            @pl.when(block > 0)
+            def _():
+                rim_copy(k + 1, 1).start()
+
+            @pl.when(block != first - 1)
+            def _():
+                late(k, layers - 1, True)
+
+                @pl.when(block < blocks - 1)
+                def _():
+                    rim_copy(k + 1, 0).start()
+
+            lax.fori_loop(1, layers - 1, body_of(late, k, False), 0)
 
     for k in range(ITERS):
         edge_copy(k, 0).wait_send()
@@ -369,14 +474,16 @@
         f32, dma = jnp.float32, pltpu.SemaphoreType.DMA
         plane = (around, lanes)
         hbm = pl.BlockSpec(memory_space=pl.ANY)
-        smem = pl.BlockSpec(memory_space=pltpu.SMEM)
         vmem = pl.BlockSpec(memory_space=pltpu.VMEM)
         return pl.pallas_call(
             functools.partial(kernel, sectors, blocks),
             out_shape=(pltpu.VMEM(prev.shape, f32),) * 2,
-            in_specs=[hbm] * 4 + [smem] * 3,
+            in_specs=[hbm] * 7,
             out_specs=(vmem, vmem),
             scratch_shapes=[
+                pltpu.SMEM(offset.shape, offset.dtype),
+                pltpu.SMEM(cells.shape, cells.dtype),
+                pltpu.SMEM(weights.shape, weights.dtype),
                 pltpu.VMEM((ITERS, comps, layers + 2) + plane, f32),
                 pltpu.VMEM(prev.shape, f32),
                 pltpu.VMEM(face.shape, face.dtype),
@@ -390,7 +497,11 @@
                 pltpu.VMEM((ITERS, comps + 1) + plane, f32),
                 [pltpu.VMEM((lows, comps + 1) + plane, f32)] * ITERS,
                 pltpu.VMEM((around + 1,) + plane, f32),
-                dma((4,)),
+                pltpu.VMEM((3, 2, comps, comps, layers, lanes), f32),
+                pltpu.VMEM((2, comps, comps, layers, lanes), f32),
+                pltpu.VMEM((2, comps, layers, lanes), f32),
+                pltpu.VMEM((2, comps, layers, lanes), f32),
+                dma((7,)),
                 dma((ITERS, 2)),
                 dma((ITERS, 2)),
                 dma((ITERS, 2)),

time: 34.5 us -> 30.9 us (0.90)
  Pallas kernels: 31.7 us -> 28.1 us
    pallas_call x1, Pallas kernels: 31.7 us -> 28.1 us  [sweeps(): pl.pallas_call(functools.partial(kernel, sectors, blocks), out_shape=(plt...]
where the time goes in v2:
time: 30.9 us; the launch traced here: 30.8 us
  Pallas kernels  28.1 us (91%)
  local copies, waits for them, and re-layouts  1.33 us (4%)
  between operations  1.29 us (4%)
    pallas_call x1, Pallas kernels, sweeps(): pl.pallas_call(functools.partial(kernel, sectors, blocks), out_shape=(plt...  28.1 us
    unnamed x2, local copies, waits for them, and re-layouts  1.33 us

profile of v2, /device:TPU:1, one launch (start us, length us, event | category | flops | bytes accessed | tf_op | source)
XLA Modules:
  0.0 30.8 jit_solution(8423270787564984158)
XLA Ops:
  1.3 28.1 %shard_map.86 = (f32[5,8,8,128]{3,2,1,0:T(8,128)S(1)}, f32[5,8,8,128]{3,2,1,0:T(8,128)S(1)}) custom-call(f32[5,8,8,128]{3,2,1,0:T(8,128)} %prev_ref.1, f32[5,8,8,128]{3,2,1,0:T(8,128)} %source_ref.1, bf16[3,5,5,8,8,128]{5,4,3,2,1,0:T(8,128)(2,1)} %face_ref.1, bf16[5,5,8,8,128]{4,3,2,1,0:T(8,128)(2,1)} %inverse_ref.1, s32[1]{0:T(128)S(6)} %copy.13.offset_hbm, ...), custom_call_target="tpu_custom_call" | custom-call | tf_op jit(solution)/shard_map/pallas_call | solution.py:478
  29.4 0.7 %copy.11 = f32[5,8,8,128]{3,2,1,0:T(8,128)} copy(f32[5,8,8,128]{3,2,1,0:T(8,128)S(1)} %get-tuple-element.2) | data formatting | bytes 327680
  30.1 0.7 %copy.12 = f32[5,8,8,128]{3,2,1,0:T(8,128)} copy(f32[5,8,8,128]{3,2,1,0:T(8,128)S(1)} %get-tuple-element.3) | data formatting | bytes 327680

commit v3 on v2

--- a/solution.py
+++ b/solution.py
@@ -335,8 +335,8 @@
             if k < ITERS - 1:
                 field[k + 1, m, a + 1] = fresh
             else:
-                adjoint_ref[m, a] = fresh
-                update_ref[m, a] = fresh - field[k, m, a + 1]
+                adjoint_ref[m, a] = 0.0 - fresh
+                update_ref[m, a] = field[k, m, a + 1]
 
     offset = offset_ref[0]
     offset_high, offset_low = offset // lows, offset % lows
@@ -475,7 +475,7 @@
         plane = (around, lanes)
         hbm = pl.BlockSpec(memory_space=pl.ANY)
         vmem = pl.BlockSpec(memory_space=pltpu.VMEM)
-        return pl.pallas_call(
+        negative, previous = pl.pallas_call(
             functools.partial(kernel, sectors, blocks),
             out_shape=(pltpu.VMEM(prev.shape, f32),) * 2,
             in_specs=[hbm] * 7,
@@ -513,6 +513,7 @@
             ],
             compiler_params=pltpu.CompilerParams(collective_id=0, has_side_effects=True),
         )(prev, source, face, inverse, offset, cells, weights)
+        return 0.0 - negative, 0.0 - negative - previous
 
     return jax.shard_map(
         sweeps,

time: 30.9 us -> 30.3 us (0.981)
  local copies, waits for them, and re-layouts: 1.33 us -> 0 us
  other arithmetic: 0 us -> 0.75 us
    unnamed x2 -> x0, local copies, waits for them, and re-layouts: 1.33 us -> none
    sub x0 -> x1, other arithmetic: none -> 0.75 us  [sweeps(): return (0.0 - negative, 0.0 - negative - previous)]
where the time goes in v3:
time: 30.3 us; the launch traced here: 30.2 us
  Pallas kernels  28.1 us (93%)
  between operations  1.29 us (4%)
  other arithmetic  0.75 us (2%)
    pallas_call x1, Pallas kernels, sweeps(): pl.pallas_call(functools.partial(kernel, sectors, blocks), out_shape=(plt...  28.1 us
    sub x1, other arithmetic, sweeps(): return (0.0 - negative, 0.0 - negative - previous)  0.75 us

profile of v3, /device:TPU:1, one launch (start us, length us, event | category | flops | bytes accessed | tf_op | source)
XLA Modules:
  0.0 30.2 jit_solution(10896114468276684625)
XLA Ops:
  1.3 28.1 %shard_map.86 = (f32[5,8,8,128]{3,2,1,0:T(8,128)S(1)}, f32[5,8,8,128]{3,2,1,0:T(8,128)S(1)}) custom-call(f32[5,8,8,128]{3,2,1,0:T(8,128)} %prev_ref.1, f32[5,8,8,128]{3,2,1,0:T(8,128)} %source_ref.1, bf16[3,5,5,8,8,128]{5,4,3,2,1,0:T(8,128)(2,1)} %face_ref.1, bf16[5,5,8,8,128]{4,3,2,1,0:T(8,128)(2,1)} %inverse_ref.1, s32[1]{0:T(128)S(6)} %copy.9.offset_hbm, ...), custom_call_target="tpu_custom_call" | custom-call | tf_op jit(solution)/shard_map/pallas_call | solution.py:478
  29.4 0.7 %fusion = (f32[5,8,8,128]{3,2,1,0:T(8,128)}, f32[5,8,8,128]{3,2,1,0:T(8,128)}) fusion(f32[5,8,8,128]{3,2,1,0:T(8,128)S(1)} %get-tuple-element.5, f32[5,8,8,128]{3,2,1,0:T(8,128)S(1)} %get-tuple-element.4), kind=kLoop, calls=%fused_computation.1 | loop fusion | flops 81920 | bytes 655360 | tf_op jit(solution)/shard_map/sub | solution.py:516
